TPU v7x, 32 devices: a whole 2x2x4 slice. The times are simulated.
32 devices in a mesh: ctx: 8 (over z, y), tp: 4 (over x, core).
Axes of the slice: x: 2, y: 2, z: 4, core: 2. Of those that a mesh axis runs over, the one named last changes fastest.
Arguments:
- queries: bfloat16 [2048, 64, 128], P('ctx', 'tp'), may hold values from -48 to 48
- keys: bfloat16 [2048, 8, 128], P('ctx', 'tp'), may hold values from -3 to 3
- values: bfloat16 [2048, 8, 128], P('ctx', 'tp'), may hold values from -6 to 6
- segment_ids: int32 [2048], P('ctx'), may hold values from 0 to 7, never falling along the last dimension, each value on 1 to 1280 neighbouring positions
Outputs:
- attended: bfloat16 [2048, 8192], P(('ctx', 'tp'))
Inputs may be any that keep to these rules, and one draw needn't show every extreme that they name: `segment_ids`: ids never fall along the tokens; each document holds 1 to 1280 tokens, and one holds exactly 1280.
All inputs are finite; a program needn't handle non-finite values.
Results may differ from a plain program's by a relative error of at most 0.003.
Values may be sent and summed in bfloat16 or wider, within the bound.
A program may use at most 64 MiB of HBM per device.

v0:
```python
import functools
import math

import jax
import jax.numpy as jnp
from jax import lax
from jax.experimental import pallas as pl
from jax.experimental.pallas import tpu as pltpu
from jax.sharding import PartitionSpec as P

MESH = pl.DeviceIdType.MESH
NEG = -1e30


def plane_width(mesh):
    n = mesh.shape["ctx"]
    try:
        width = len({d.coords[1] for d in mesh.devices.flat})
    except Exception:
        width = 2
    return width if n % width == 0 else 1


def kernel(cfg, q_in, k_in, v_in, seg_ref, out_ref,
           q_ref, buf, segs, segcol, bias, acc, top, o_buf,
           kv_send, kv_recv, seg_send, seg_recv, o_send, o_recv, o_local):
    n, ny, reach, tp, groups, per_group, rows, head = cfg
    nz = n // ny
    depth = min(nz - 1, (reach + ny - 1) // ny) + 1
    out_rows = rows // tp
    const = math.log2(math.e) / math.sqrt(head)
    me = lax.axis_index("ctx")
    mt = lax.axis_index("tp")
    z = me // ny
    y = me % ny

    barrier = pltpu.get_barrier_semaphore()
    for d in range(1, reach + 1):
        @pl.when(me + d < n)
        def _():
            pl.semaphore_signal(barrier, inc=1, device_id={"ctx": me + d, "tp": mt}, device_id_type=MESH)

        @pl.when(me - d >= 0)
        def _():
            pl.semaphore_signal(barrier, inc=1, device_id={"ctx": me - d, "tp": mt}, device_id_type=MESH)
    for e in range(1, tp):
        pl.semaphore_signal(barrier, inc=1, device_id={"ctx": me, "tp": (mt + e) % tp}, device_id_type=MESH)
    peers = (tp - 1) + jnp.minimum(n - 1 - me, reach) + jnp.minimum(me, reach)
    pl.semaphore_wait(barrier, peers)

    def piece(s, dy, g, w):
        if s == 0 and dy == 0:
            return (k_in, v_in)[w].at[g]
        return buf.at[s * ny + dy, g, w]

    def sem_index(s, dy, g, w):
        return ((s * ny + dy) * groups + g) * 2 + w

    def send_index(s, e, g, w):
        return ((s * ny + e) * groups + g) * 2 + w

    def z_copy(s, g, w):
        return pltpu.make_async_remote_copy(
            src_ref=piece(s, 0, g, w),
            dst_ref=buf.at[(s + 1) * ny, g, w],
            send_sem=kv_send.at[send_index(s, 0, g, w)],
            recv_sem=kv_recv.at[sem_index(s + 1, 0, g, w)],
            device_id={"ctx": me + ny, "tp": mt},
            device_id_type=MESH,
        )

    def y_copy(s, e, g, w):
        return pltpu.make_async_remote_copy(
            src_ref=piece(s, 0, g, w),
            dst_ref=buf.at[s * ny + ny - e, g, w],
            send_sem=kv_send.at[send_index(s, e, g, w)],
            recv_sem=kv_recv.at[sem_index(s, ny - e, g, w)],
            device_id={"ctx": z * ny + (y + e) % ny, "tp": mt},
            device_id_type=MESH,
        )

    last = depth - 1
    straight = last >= 2 and last * ny > reach

    def far_copy(dy, g, w):
        return pltpu.make_async_remote_copy(
            src_ref=piece(last - 1, dy, g, w),
            dst_ref=buf.at[last * ny + dy, g, w],
            send_sem=kv_send.at[send_index(last, dy, g, w)],
            recv_sem=kv_recv.at[sem_index(last, dy, g, w)],
            device_id={"ctx": me + ny, "tp": mt},
            device_id_type=MESH,
        )

    def sends_far(dy):
        gap = me + ny - owner(last - 1, dy)
        return (z >= last - 1) & (z + 1 < nz) & (gap <= reach)

    def owner(s, dy):
        return (z - s) * ny + (y + dy) % ny

    def has_column(s):
        return (z >= s) & (s * ny <= reach)

    def sends_z(s):
        return (z >= s) & (z + 1 < nz) & ((s + 1) * ny <= reach)

    def sends_y(s, e):
        gap = z * ny + (y + e) % ny - owner(s, 0)
        return (z >= s) & (s * ny <= reach) & (gap > 0) & (gap <= reach)

    def wanted(s, dy):
        gap = me - owner(s, dy)
        return (z >= s) & (gap > 0) & (gap <= reach)

    def arrived(s, dy, g, w):
        pltpu.make_async_copy(buf.at[s * ny + dy, g, w], buf.at[s * ny + dy, g, w],
                              kv_recv.at[sem_index(s, dy, g, w)]).wait()

    def push(s, g):
        for w in range(2):
            if s > 0:
                @pl.when(has_column(s))
                def _():
                    arrived(s, 0, g, w)
            if s + 1 < depth:
                @pl.when(sends_z(s))
                def _():
                    z_copy(s, g, w).start()
            for e in range(1, ny):
                @pl.when(sends_y(s, e))
                def _():
                    y_copy(s, e, g, w).start()

    def seg_copy(d):
        return pltpu.make_async_remote_copy(
            src_ref=seg_ref,
            dst_ref=segs.at[d],
            send_sem=seg_send.at[d],
            recv_sem=seg_recv.at[d],
            device_id={"ctx": me + d, "tp": mt},
            device_id_type=MESH,
        )

    push(0, 0)
    for d in range(1, reach + 1):
        @pl.when(me + d < n)
        def _():
            seg_copy(d).start()

    for i in range(groups * per_group):
        q_ref[i] = q_in[:, i, :]
    segcol[...] = jnp.transpose(jnp.broadcast_to(seg_ref[...], (head, rows)))

    def attend(s, dy, g, first):
        k_ref, v_ref = piece(s, dy, g, 0), piece(s, dy, g, 1)
        if first:
            seg_k = seg_ref[...]
        else:
            seg_k = segs[me - owner(s, dy)]
        column = segcol[...]
        allowed = jnp.concatenate([column] * (rows // head), axis=1) == seg_k
        if first:
            r = lax.broadcasted_iota(jnp.int32, (rows, rows), 0)
            c = lax.broadcasted_iota(jnp.int32, (rows, rows), 1)
            allowed = allowed & (c <= r)
        bias[...] = jnp.where(allowed, 0.0, NEG)

        def one(h, carry):
            i = g * per_group + h
            scores = lax.dot_general(q_ref[i], k_ref[...], (((1,), (1,)), ((), ())),
                                     preferred_element_type=jnp.float32)
            scores = scores * const + bias[...]
            high = jnp.broadcast_to(jnp.max(scores, axis=1, keepdims=True), (rows, head))
            if not first:
                old = top[i]
                high = jnp.maximum(old, high)
            weights = jnp.exp2(scores - jnp.concatenate([high] * (rows // head), axis=1)).astype(jnp.bfloat16)
            v = jnp.concatenate([v_ref[...], jnp.ones((rows, head), jnp.bfloat16)], axis=1)
            mixed = jnp.dot(weights, v, preferred_element_type=jnp.float32)
            if not first:
                factor = jnp.exp2(old - high)
                mixed = acc[i] * jnp.concatenate([factor, factor], axis=1) + mixed
            acc[i] = mixed
            top[i] = high
            return carry

        lax.fori_loop(0, per_group, one, 0, unroll=per_group)

    def attend_y(s, g):
        for dy in range(1, ny):
            @pl.when(wanted(s, dy))
            def _():
                arrived(s, dy, g, 0)
                arrived(s, dy, g, 1)
                if straight and s == last - 1:
                    @pl.when(sends_far(dy))
                    def _():
                        far_copy(dy, g, 0).start()
                        far_copy(dy, g, 1).start()
                attend(s, dy, g, False)

    per_send = max(per_group // 2, 1)
    width = per_send * head
    pieces = per_group // per_send

    def o_copy(c, e):
        col = pl.multiple_of((mt * groups * pieces + c) * width, width)
        to = (mt + e) % tp
        return pltpu.make_async_remote_copy(
            src_ref=o_buf.at[pl.ds(pl.multiple_of(to * out_rows, out_rows), out_rows), pl.ds(c * width, width)],
            dst_ref=out_ref.at[:, pl.ds(col, width)],
            send_sem=o_send.at[c * tp + e],
            recv_sem=o_recv.at[c * tp + e],
            device_id={"ctx": me, "tp": to},
            device_id_type=MESH,
        )

    def o_own(c):
        col = pl.multiple_of((mt * groups * pieces + c) * width, width)
        return pltpu.make_async_copy(
            o_buf.at[pl.ds(pl.multiple_of(mt * out_rows, out_rows), out_rows), pl.ds(c * width, width)],
            out_ref.at[:, pl.ds(col, width)],
            o_local.at[c],
        )

    def finish(g):
        for p in range(pieces):
            c = g * pieces + p
            for h in range(per_send):
                i = g * per_group + p * per_send + h
                o_buf[:, i * head:(i + 1) * head] = (acc[i, :, :head] / acc[i, :, head:]).astype(jnp.bfloat16)
            for e in range(1, tp):
                o_copy(c, e).start()
            o_own(c).start()

    for g in range(groups):
        attend(0, 0, g, True)
        if g == 0:
            for d in range(1, reach + 1):
                @pl.when(me - d >= 0)
                def _():
                    pltpu.make_async_copy(segs.at[d], segs.at[d], seg_recv.at[d]).wait()
        for s in range(1, depth):
            push(s, g)
            if s == depth - 1 and g + 1 < groups:
                push(0, g + 1)

            @pl.when(wanted(s, 0))
            def _():
                attend(s, 0, g, False)
            attend_y(s - 1, g)
        if depth == 1 and g + 1 < groups:
            push(0, g + 1)
        attend_y(depth - 1, g)
        finish(g)

    for s in range(depth):
        for g in range(groups):
            for w in range(2):
                if s + 1 < depth:
                    @pl.when(sends_z(s))
                    def _():
                        z_copy(s, g, w).wait_send()
                for e in range(1, ny):
                    @pl.when(sends_y(s, e))
                    def _():
                        y_copy(s, e, g, w).wait_send()
    if straight:
        for g in range(groups):
            for w in range(2):
                for dy in range(1, ny):
                    @pl.when(wanted(last - 1, dy) & sends_far(dy))
                    def _():
                        far_copy(dy, g, w).wait_send()
    for d in range(1, reach + 1):
        @pl.when(me + d < n)
        def _():
            seg_copy(d).wait_send()
    for c in range(groups * pieces):
        o_own(c).wait()
        for e in range(1, tp):
            o_copy(c, e).wait()


def local(ny, queries, keys, values, segment_ids):
    rows, heads, head = queries.shape
    groups = keys.shape[1]
    per_group = heads // groups
    n = lax.axis_size("ctx")
    tp = lax.axis_size("tp")
    nz = n // ny
    longest = rows * n * 5 // 8
    reach = min((longest + rows - 1) // rows, n - 1)
    depth = min(nz - 1, (reach + ny - 1) // ny) + 1
    k = jnp.transpose(keys, (1, 0, 2))
    v = jnp.transpose(values, (1, 0, 2))
    pieces = groups * (per_group // max(per_group // 2, 1))
    slots = depth * ny
    vmem = pl.BlockSpec(memory_space=pltpu.VMEM)
    dma = pltpu.SemaphoreType.DMA
    cfg = (n, ny, reach, tp, groups, per_group, rows, head)
    return pl.pallas_call(
        functools.partial(kernel, cfg),
        out_shape=jax.ShapeDtypeStruct((rows // tp, tp * heads * head), jnp.bfloat16),
        in_specs=[vmem] * 4,
        out_specs=vmem,
        scratch_shapes=[
            pltpu.VMEM((heads, rows, head), jnp.bfloat16),
            pltpu.VMEM((slots, groups, 2, rows, head), jnp.bfloat16),
            pltpu.VMEM((reach + 1, 1, rows), jnp.int32),
            pltpu.VMEM((rows, head), jnp.int32),
            pltpu.VMEM((rows, rows), jnp.float32),
            pltpu.VMEM((heads, rows, 2 * head), jnp.float32),
            pltpu.VMEM((heads, rows, head), jnp.float32),
            pltpu.VMEM((rows, heads * head), jnp.bfloat16),
            dma((slots * groups * 2,)),
            dma((slots * groups * 2,)),
            dma((reach + 1,)),
            dma((reach + 1,)),
            dma((pieces * tp,)),
            dma((pieces * tp,)),
            dma((pieces,)),
        ],
        compiler_params=pltpu.CompilerParams(
            collective_id=0, has_side_effects=True, vmem_limit_bytes=56 * 1024 * 1024
        ),
    )(queries, k, v, segment_ids.reshape(1, rows))


def solution(mesh):
    in_specs = (P("ctx", "tp", None), P("ctx", "tp", None), P("ctx", "tp", None), P("ctx"))
    out_specs = P(("ctx", "tp"), None)
    body = functools.partial(local, plane_width(mesh))
    return jax.shard_map(body, mesh=mesh, in_specs=in_specs, out_specs=out_specs, check_vma=False)
```

profile of v0, /device:TPU:25, one launch (start us, length us, event | category | flops | bytes accessed | tf_op | source)
XLA Modules:
  0.0 41.7 jit_solution(10725232607453252559)
XLA Ops:
  0.0 1.7 %copy_bitcast_fusion = (bf16[2,256,128]{2,1,0:T(8,128)(2,1)}, bf16[2,256,128]{2,1,0:T(8,128)(2,1)}) fusion(bf16[256,2,128]{2,1,0:T(2,128)(2,1)} %param.6, bf16[256,2,128]{2,1,0:T(2,128)(2,1)} %param.5), kind=kLoop, calls=%fused_computation | loop fusion | bytes 524288 | tf_op jit(solution)/shard_map/transpose | solution.py:297
  1.7 37.8 %shard_map.46 = bf16[64,8192]{1,0:T(8,128)(2,1)} custom-call(bf16[256,16,128]{2,1,0:T(8,128)(2,1)} %q_in.1, bf16[2,256,128]{2,1,0:T(8,128)(2,1)} %get-tuple-element.6.k_in, bf16[2,256,128]{2,1,0:T(8,128)(2,1)} %get-tuple-element.5.v_in, s32[1,256]{1,0:T(1,128)} %bitcast.5), custom_call_target="tpu_custom_call" | custom-call | tf_op jit(solution)/shard_map/pallas_call | solution.py:303
  39.5 2.3 %copy.10 = bf16[64,8192]{1,0:T(8,128)(2,1)} copy(bf16[64,8192]{1,0:T(8,128)(2,1)} %shard_map.46) | data formatting | bytes 2097152
where the time goes:
time: 41.9 us; the launch traced here: 41.7 us
  Pallas kernels  37.8 us (90%)
  local copies, waits for them, and re-layouts  3.96 us (9%)
    pallas_call x1, Pallas kernels, local(): pl.pallas_call(functools.partial(kernel, cfg), out_shape=jax.ShapeDtypeSt...  37.8 us
    unnamed x1, local copies, waits for them, and re-layouts  2.26 us
    transpose x1, local copies, waits for them, and re-layouts, local(): v = jnp.transpose(values, (1, 0, 2))  1.7 us

commit v1 on v0

--- a/solution.py
+++ b/solution.py
@@ -302,7 +302,7 @@
     cfg = (n, ny, reach, tp, groups, per_group, rows, head)
     return pl.pallas_call(
         functools.partial(kernel, cfg),
-        out_shape=jax.ShapeDtypeStruct((rows // tp, tp * heads * head), jnp.bfloat16),
+        out_shape=pltpu.VMEM((rows // tp, tp * heads * head), jnp.bfloat16),
         in_specs=[vmem] * 4,
         out_specs=vmem,
         scratch_shapes=[

time: 41.9 us -> 39.6 us (0.945)
  local copies, waits for them, and re-layouts: 3.96 us -> 2.67 us
  Pallas kernels: 37.8 us -> 36.8 us
    unnamed x1, local copies, waits for them, and re-layouts: 2.26 us -> 0.97 us
    pallas_call x1, Pallas kernels: 37.8 us -> 36.8 us  [local(): pl.pallas_call(functools.partial(kernel, cfg), out_shape=pltpu.VMEM((rows...]
where the time goes in v1:
time: 39.6 us; the launch traced here: 39.5 us
  Pallas kernels  36.8 us (93%)
  local copies, waits for them, and re-layouts  2.67 us (7%)
    pallas_call x1, Pallas kernels, local(): pl.pallas_call(functools.partial(kernel, cfg), out_shape=pltpu.VMEM((rows...  36.8 us
    transpose x1, local copies, waits for them, and re-layouts, local(): v = jnp.transpose(values, (1, 0, 2))  1.7 us
    unnamed x1, local copies, waits for them, and re-layouts  0.97 us

profile of v1, /device:TPU:25, one launch (start us, length us, event | category | flops | bytes accessed | tf_op | source)
XLA Modules:
  0.0 39.5 jit_solution(2101036873804658045)
XLA Ops:
  0.0 1.7 %copy_bitcast_fusion = (bf16[2,256,128]{2,1,0:T(8,128)(2,1)}, bf16[2,256,128]{2,1,0:T(8,128)(2,1)}) fusion(bf16[256,2,128]{2,1,0:T(2,128)(2,1)} %param.6, bf16[256,2,128]{2,1,0:T(2,128)(2,1)} %param.5), kind=kLoop, calls=%fused_computation | loop fusion | bytes 524288 | tf_op jit(solution)/shard_map/transpose | solution.py:297
  1.7 36.8 %shard_map.46 = bf16[64,8192]{1,0:T(8,128)(2,1)S(1)} custom-call(bf16[256,16,128]{2,1,0:T(8,128)(2,1)} %q_in.1, bf16[2,256,128]{2,1,0:T(8,128)(2,1)} %get-tuple-element.6.k_in, bf16[2,256,128]{2,1,0:T(8,128)(2,1)} %get-tuple-element.5.v_in, s32[1,256]{1,0:T(1,128)} %bitcast.5), custom_call_target="tpu_custom_call" | custom-call | tf_op jit(solution)/shard_map/pallas_call | solution.py:303
  38.5 1.0 %copy.10 = bf16[64,8192]{1,0:T(8,128)(2,1)} copy(bf16[64,8192]{1,0:T(8,128)(2,1)S(1)} %shard_map.46) | data formatting | bytes 2097152

commit v2 on v1

--- a/solution.py
+++ b/solution.py
@@ -328,8 +328,426 @@
     )(queries, k, v, segment_ids.reshape(1, rows))
 
 
+UNITS = (
+    (0, 0, 0, 0, 0, 0, 0, 0),
+    (0, 0, 0, 0, 0, 0, 0, 0),
+    (0, 0, 16, 16, 18, 19, 20, 21),
+    (0, 0, 0, 18, 19, 27, 21, 22),
+    (0, 0, 0, 0, 16, 20, 18, 19),
+    (0, 0, 0, 0, 0, 28, 28, 20),
+    (0, 0, 0, 0, 0, 18, 19, 0),
+    (0, 0, 0, 0, 0, 16, 0, 0),
+    (0, 16, 17, 17, 17, 17, 17, 18),
+    (0, 0, 24, 26, 27, 26, 26, 28),
+    (0, 0, 0, 24, 26, 24, 29, 29),
+    (0, 0, 0, 0, 25, 0, 25, 27),
+    (0, 0, 0, 0, 0, 0, 0, 30),
+    (0, 24, 25, 25, 24, 25, 27, 26),
+)
+EVENTS = (
+    (
+        (2152, 2209, 2170, 2091, 2172, 2101, 2118, 0),
+        (2144, 2217, 2154, 2083, 0, 2085, 0, 0),
+        (0, 0, 2146, 2099, 0, 2093, 0, 0),
+        (0, 0, 2144, 0, 0, 0, 0, 0),
+        (0, 0, 2152, 0, 0, 0, 0, 0),
+    ),
+    (
+        (0, 0, 0, 2107, 2148, 2147, 2140, 0),
+        (0, 0, 0, 0, 2164, 0, 2116, 0),
+        (0, 0, 0, 0, 2156, 0, 0, 0),
+    ),
+    (
+        (2160, 2233, 2081, 2089, 0, 2155, 2126, 2133),
+        (0, 0, 2136, 0, 0, 0, 0, 0),
+    ),
+    (
+        (0, 0, 0, 2058, 2154, 2109, 0, 2054),
+        (0, 0, 0, 2050, 2112, 2163, 0, 2117),
+        (0, 0, 0, 2048, 2146, 0, 0, 0),
+        (0, 0, 0, 2074, 0, 0, 0, 0),
+        (0, 0, 0, 2105, 0, 0, 0, 0),
+        (0, 0, 0, 2088, 0, 0, 0, 0),
+    ),
+    (
+        (2168, 2056, 0, 0, 2170, 2060, 2124, 2125),
+        (0, 0, 0, 0, 0, 2052, 2058, 2052),
+        (0, 0, 0, 0, 0, 2171, 0, 2115),
+    ),
+    (
+        (0, 2225, 2089, 2104, 2056, 0, 2053, 2076),
+        (0, 0, 0, 0, 2059, 0, 2069, 0),
+        (0, 0, 0, 0, 2051, 0, 0, 0),
+    ),
+    (
+        (0, 2048, 2162, 0, 2145, 0, 2132, 2062),
+        (0, 0, 0, 0, 0, 0, 2114, 2123),
+        (0, 0, 0, 0, 0, 0, 2061, 0),
+    ),
+    (
+        (0, 0, 0, 0, 0, 0, 0, 2060),
+        (0, 0, 0, 0, 0, 0, 0, 2141),
+    ),
+    (
+        (0, 0, 0, 2065, 0, 2076, 0, 0),
+    ),
+    (
+        (0, 0, 0, 2049, 2089, 0, 2134, 0),
+        (0, 0, 0, 0, 2067, 0, 0, 0),
+        (0, 0, 0, 0, 2162, 0, 0, 0),
+    ),
+    (
+        (0, 0, 0, 0, 0, 2090, 0, 2139),
+        (0, 0, 0, 0, 0, 2137, 0, 0),
+        (0, 0, 0, 0, 0, 2068, 0, 0),
+        (0, 0, 0, 0, 0, 2048, 0, 0),
+    ),
+    (
+        (0, 0, 0, 0, 0, 0, 0, 2131),
+        (0, 0, 0, 0, 0, 0, 0, 2050),
+        (0, 0, 0, 0, 0, 0, 0, 2068),
+    ),
+    (
+        (0, 0, 0, 0, 0, 2050, 2051, 2058),
+        (0, 0, 0, 0, 0, 2056, 2142, 0),
+        (0, 0, 0, 0, 0, 0, 2059, 0),
+    ),
+    (),
+    (
+        (0, 0, 0, 0, 0, 0, 2057, 0),
+    ),
+    (
+        (0, 0, 0, 0, 0, 0, 2049, 0),
+    ),
+    (
+        (0, 0, 0, 0, 0, 2057, 0, 0),
+        (0, 0, 0, 0, 0, 2074, 0, 0),
+        (0, 0, 0, 0, 0, 2136, 0, 0),
+        (0, 0, 0, 0, 0, 2049, 0, 0),
+    ),
+    (
+        (0, 0, 2160, 0, 2075, 2064, 2138, 0),
+    ),
+    (
+        (0, 2072, 0, 2066, 2128, 2066, 2130, 0),
+        (0, 0, 0, 2064, 2105, 0, 2077, 0),
+    ),
+    (
+        (0, 2064, 0, 0, 0, 0, 0, 0),
+    ),
+    (
+        (0, 0, 2097, 0, 2161, 0, 2075, 0),
+        (0, 0, 0, 0, 0, 0, 2073, 0),
+    ),
+    (
+        (0, 0, 2073, 0, 0, 0, 0, 0),
+    ),
+    (
+        (0, 0, 0, 0, 0, 2065, 2067, 0),
+        (0, 0, 0, 0, 0, 0, 2065, 0),
+    ),
+    (
+        (0, 0, 0, 0, 2072, 0, 0, 2070),
+    ),
+    (
+        (0, 0, 0, 0, 0, 0, 0, 2078),
+        (0, 0, 0, 0, 0, 0, 0, 2074),
+    ),
+    (
+        (0, 0, 0, 0, 0, 0, 0, 2066),
+    ),
+    (),
+    (),
+    (),
+)
+LAST = (8, 13)
+
+
+def targets(code, me):
+    found = []
+    if code // 2048 % 2:
+        if code // 32 % 2:
+            found.append(me + 2)
+        if code // 64 % 2:
+            found.append(me ^ 1)
+        if code // 128 % 8:
+            found.append(me + code // 128 % 8)
+    return found
+
+
+def planned_kernel(cfg, q_hbm, k_hbm, v_hbm, seg_hbm, out_ref,
+                   q_raw, kv_raw, q_ref, buf, segs, segcol, bias, acc, top, o_buf,
+                   load, kv_send, kv_recv, seg_send, seg_recv, o_send, o_recv):
+    n, tp, groups, per_group, rows, head = cfg
+    out_rows = rows // tp
+    const = math.log2(math.e) / math.sqrt(head)
+    me = lax.axis_index("ctx")
+    mt = lax.axis_index("tp")
+
+    def pick(values):
+        usual = max(set(values), key=values.count)
+        chosen = jnp.int32(usual)
+        for d, value in enumerate(values):
+            if value != usual:
+                chosen = jnp.where(me == d, jnp.int32(value), chosen)
+        return chosen
+
+    k_load = pltpu.make_async_copy(k_hbm, kv_raw.at[0], load.at[0])
+    v_load = pltpu.make_async_copy(v_hbm, kv_raw.at[1], load.at[1])
+    seg_load = pltpu.make_async_copy(seg_hbm, segs.at[me], load.at[2])
+    q_load = pltpu.make_async_copy(q_hbm, q_raw, load.at[3])
+    k_load.start()
+    v_load.start()
+    seg_load.start()
+    q_load.start()
+
+    edges = sorted({(m, t) for step in EVENTS for slot in step for m, code in enumerate(slot) for t in targets(code, m)})
+    barrier = pltpu.get_barrier_semaphore()
+    for s, d in edges:
+        @pl.when(me == d)
+        def _():
+            pl.semaphore_signal(barrier, inc=1, device_id={"ctx": s, "tp": mt}, device_id_type=MESH)
+    for e in range(1, tp):
+        pl.semaphore_signal(barrier, inc=1, device_id={"ctx": me, "tp": (mt + e) % tp}, device_id_type=MESH)
+    k_load.wait()
+    v_load.wait()
+    for w in range(2):
+        for g in range(groups):
+            buf[me, g, w] = kv_raw[w, :, g, :]
+    seg_load.wait()
+    pl.semaphore_wait(barrier, pick([sum(s == m for s, _ in edges) for m in range(n)]) + (tp - 1))
+
+    def piece_copy(b, gw, way, to):
+        index = b * (2 * groups) + gw
+        return pltpu.make_async_remote_copy(
+            src_ref=buf.at[b, gw // 2, gw % 2],
+            dst_ref=buf.at[b, gw // 2, gw % 2],
+            send_sem=kv_send.at[index * 3 + way],
+            recv_sem=kv_recv.at[index],
+            device_id={"ctx": to, "tp": mt},
+            device_id_type=MESH,
+        )
+
+    def seg_copy(b, way, to):
+        return pltpu.make_async_remote_copy(
+            src_ref=segs.at[b],
+            dst_ref=segs.at[b],
+            send_sem=seg_send.at[b * 3 + way],
+            recv_sem=seg_recv.at[b],
+            device_id={"ctx": to, "tp": mt},
+            device_id_type=MESH,
+        )
+
+    def routes(slot):
+        code = pick(slot)
+        b, gw, far = code % 8, code // 8 % 4, code // 128 % 8
+        ways = []
+        if any(v // 32 % 2 for v in slot):
+            ways.append((0, code // 32 % 2 == 1, me + 2))
+        if any(v // 64 % 2 for v in slot):
+            ways.append((1, code // 64 % 2 == 1, me + 1 - 2 * (me % 2)))
+        if any(v // 128 % 8 for v in slot):
+            ways.append((2, far > 0, me + far))
+        return code, b, gw, ways
+
+    def event(slot):
+        code, b, gw, ways = routes(slot)
+        head_piece = any(v // 2048 and v // 8 % 4 == 0 for v in slot)
+
+        @pl.when(code // 2048 == 1)
+        def _():
+            @pl.when(b != me)
+            def _():
+                pltpu.make_async_copy(buf.at[b, gw // 2, gw % 2], buf.at[b, gw // 2, gw % 2],
+                                      kv_recv.at[b * (2 * groups) + gw]).wait()
+            for way, on, to in ways:
+                @pl.when(on)
+                def _():
+                    piece_copy(b, gw, way, to).start()
+            if head_piece:
+                @pl.when(gw == 0)
+                def _():
+                    @pl.when(b != me)
+                    def _():
+                        pltpu.make_async_copy(segs.at[b], segs.at[b], seg_recv.at[b]).wait()
+                    for way, on, to in ways:
+                        @pl.when(on)
+                        def _():
+                            seg_copy(b, way, to).start()
+
+    def drain(slot):
+        code, b, gw, ways = routes(slot)
+        head_piece = any(v // 2048 and v // 8 % 4 == 0 for v in slot)
+
+        @pl.when(code // 2048 == 1)
+        def _():
+            for way, on, to in ways:
+                @pl.when(on)
+                def _():
+                    piece_copy(b, gw, way, to).wait_send()
+            if head_piece:
+                @pl.when(gw == 0)
+                def _():
+                    for way, on, to in ways:
+                        @pl.when(on)
+                        def _():
+                            seg_copy(b, way, to).wait_send()
+
+    def one(g, h, k_ref, v_ref, first):
+        i = g * per_group + h
+        scores = lax.dot_general(q_ref[i], k_ref[...], (((1,), (1,)), ((), ())),
+                                 preferred_element_type=jnp.float32)
+        scores = scores * const + bias[...]
+        high = jnp.broadcast_to(jnp.max(scores, axis=1, keepdims=True), (rows, head))
+        if not first:
+            old = top[i]
+            high = jnp.maximum(old, high)
+        weights = jnp.exp2(scores - jnp.concatenate([high] * (rows // head), axis=1)).astype(jnp.bfloat16)
+        v = jnp.concatenate([v_ref[...], jnp.ones((rows, head), jnp.bfloat16)], axis=1)
+        mixed = jnp.dot(weights, v, preferred_element_type=jnp.float32)
+        if not first:
+            factor = jnp.exp2(old - high)
+            mixed = acc[i] * jnp.concatenate([factor, factor], axis=1) + mixed
+        acc[i] = mixed
+        top[i] = high
+
+    def set_bias(b, first):
+        allowed = jnp.concatenate([segcol[...]] * (rows // head), axis=1) == segs[b]
+        if first:
+            r = lax.broadcasted_iota(jnp.int32, (rows, rows), 0)
+            c = lax.broadcasted_iota(jnp.int32, (rows, rows), 1)
+            allowed = allowed & (c <= r)
+        bias[...] = jnp.where(allowed, 0.0, NEG)
+
+    def unit(values, half):
+        code = pick(values)
+        b, g = code % 8, code // 8 % 2
+
+        @pl.when(code // 16 == 1)
+        def _():
+            if half == 0:
+                set_bias(b, False)
+            for h in halves[half]:
+                one(g, h, buf.at[b, g, 0], buf.at[b, g, 1], False)
+
+    halves = (range(per_group // 2), range(per_group // 2, per_group))
+    per_send = 2
+    width = per_send * head
+    pieces = per_group // per_send
+
+    def o_copy(c, e):
+        col = pl.multiple_of((mt * groups * pieces + c) * width, width)
+        to = (mt + e) % tp
+        return pltpu.make_async_remote_copy(
+            src_ref=o_buf.at[pl.ds(pl.multiple_of(to * out_rows, out_rows), out_rows), pl.ds(c * width, width)],
+            dst_ref=out_ref.at[:, pl.ds(col, width)],
+            send_sem=o_send.at[c * tp + e],
+            recv_sem=o_recv.at[c * tp + e],
+            device_id={"ctx": me, "tp": to},
+            device_id_type=MESH,
+        )
+
+    def last_unit(values, g, half):
+        code = pick(values)
+        b = code % 8
+        live = code // 16 == 1
+
+        if half == 0:
+            @pl.when(live)
+            def _():
+                set_bias(b, False)
+        for p in range(half * pieces // 2, (half + 1) * pieces // 2):
+            @pl.when(live)
+            def _():
+                for h in range(per_send):
+                    one(g, p * per_send + h, buf.at[b, g, 0], buf.at[b, g, 1], False)
+            c = g * pieces + p
+            for h in range(per_send):
+                i = g * per_group + p * per_send + h
+                o_buf[:, i * head:(i + 1) * head] = (acc[i, :, :head] / acc[i, :, head:]).astype(jnp.bfloat16)
+            for e in range(1, tp):
+                o_copy(c, e).start()
+            mine = pl.ds(pl.multiple_of(mt * out_rows, out_rows), out_rows)
+            col = pl.multiple_of((mt * groups * pieces + c) * width, width)
+            out_ref[:, pl.ds(col, width)] = o_buf[mine, c * width:(c + 1) * width]
+
+    for slot in EVENTS[0]:
+        event(slot)
+    q_load.wait()
+    segcol[...] = jnp.transpose(jnp.broadcast_to(segs[me], (head, rows)))
+    set_bias(me, True)
+    for step, values in enumerate(UNITS):
+        for half in range(2):
+            if step + half > 0:
+                for slot in EVENTS[2 * step + half]:
+                    event(slot)
+            if step < groups:
+                for h in halves[half]:
+                    q_ref[step * per_group + h] = q_raw[:, step * per_group + h, :]
+                for h in halves[half]:
+                    one(step, h, buf.at[me, step, 0], buf.at[me, step, 1], True)
+            elif step in LAST:
+                last_unit(values, LAST.index(step), half)
+            else:
+                unit(values, half)
+    for slot in EVENTS[2 * len(UNITS)]:
+        event(slot)
+
+    for group in EVENTS:
+        for slot in group:
+            drain(slot)
+    for c in range(groups * pieces):
+        for e in range(1, tp):
+            o_copy(c, e).wait()
+
+
+def planned(queries, keys, values, segment_ids):
+    rows, heads, head = queries.shape
+    groups = keys.shape[1]
+    per_group = heads // groups
+    n = lax.axis_size("ctx")
+    tp = lax.axis_size("tp")
+    chunks = groups * per_group // 2
+    hbm = pl.BlockSpec(memory_space=pltpu.HBM)
+    dma = pltpu.SemaphoreType.DMA
+    cfg = (n, tp, groups, per_group, rows, head)
+    return pl.pallas_call(
+        functools.partial(planned_kernel, cfg),
+        out_shape=pltpu.VMEM((rows // tp, tp * heads * head), jnp.bfloat16),
+        in_specs=[hbm] * 4,
+        out_specs=pl.BlockSpec(memory_space=pltpu.VMEM),
+        scratch_shapes=[
+            pltpu.VMEM((rows, heads, head), jnp.bfloat16),
+            pltpu.VMEM((2, rows, groups, head), jnp.bfloat16),
+            pltpu.VMEM((heads, rows, head), jnp.bfloat16),
+            pltpu.VMEM((n, groups, 2, rows, head), jnp.bfloat16),
+            pltpu.VMEM((n, 1, rows), jnp.int32),
+            pltpu.VMEM((rows, head), jnp.int32),
+            pltpu.VMEM((rows, rows), jnp.float32),
+            pltpu.VMEM((heads, rows, 2 * head), jnp.float32),
+            pltpu.VMEM((heads, rows, head), jnp.float32),
+            pltpu.VMEM((rows, heads * head), jnp.bfloat16),
+            dma((4,)),
+            dma((n * groups * 2 * 3,)),
+            dma((n * groups * 2,)),
+            dma((n * 3,)),
+            dma((n,)),
+            dma((chunks * tp,)),
+            dma((chunks * tp,)),
+        ],
+        compiler_params=pltpu.CompilerParams(
+            collective_id=0, has_side_effects=True, vmem_limit_bytes=56 * 1024 * 1024
+        ),
+    )(queries, keys, values, segment_ids.reshape(1, rows))
+
+
+def fits_plan(mesh):
+    n = mesh.shape["ctx"]
+    return plane_width(mesh) == 2 and n == len(UNITS[0])
+
+
 def solution(mesh):
     in_specs = (P("ctx", "tp", None), P("ctx", "tp", None), P("ctx", "tp", None), P("ctx"))
     out_specs = P(("ctx", "tp"), None)
-    body = functools.partial(local, plane_width(mesh))
+    body = planned if fits_plan(mesh) else functools.partial(local, plane_width(mesh))
     return jax.shard_map(body, mesh=mesh, in_specs=in_specs, out_specs=out_specs, check_vma=False)

time: 39.6 us -> 35 us (0.88)
  Pallas kernels: 36.8 us -> 33.8 us
  local copies, waits for them, and re-layouts: 2.67 us -> 0.97 us
    pallas_call x1, Pallas kernels: 36.8 us -> 33.8 us  [planned(): pl.pallas_call(functools.partial(planned_kernel, cfg), out_shape=pltpu.VM...]
    transpose x1 -> x0, local copies, waits for them, and re-layouts: 1.7 us -> none  [local(): v = jnp.transpose(values, (1, 0, 2))]
where the time goes in v2:
time: 35 us; the launch traced here: 34.8 us
  Pallas kernels  33.8 us (97%)
  local copies, waits for them, and re-layouts  0.97 us (3%)
    pallas_call x1, Pallas kernels, planned(): pl.pallas_call(functools.partial(planned_kernel, cfg), out_shape=pltpu.VM...  33.8 us
    unnamed x1, local copies, waits for them, and re-layouts  0.97 us

profile of v2, /device:TPU:25, one launch (start us, length us, event | category | flops | bytes accessed | tf_op | source)
XLA Modules:
  0.0 34.8 jit_solution(7823464082746303717)
XLA Ops:
  0.0 33.8 %shard_map.46 = bf16[64,8192]{1,0:T(8,128)(2,1)S(1)} custom-call(bf16[256,16,128]{2,1,0:T(8,128)(2,1)} %q_hbm.1, bf16[256,2,128]{2,1,0:T(2,128)(2,1)} %k_hbm.1, bf16[256,2,128]{2,1,0:T(2,128)(2,1)} %v_hbm.1, s32[1,256]{1,0:T(1,128)} %bitcast.1), custom_call_target="tpu_custom_call" | custom-call | tf_op jit(solution)/shard_map/pallas_call | solution.py:714
  33.8 1.0 %copy.6 = bf16[64,8192]{1,0:T(8,128)(2,1)} copy(bf16[64,8192]{1,0:T(8,128)(2,1)S(1)} %shard_map.46) | data formatting | bytes 2097152

commit v3 on v2

--- a/solution.py
+++ b/solution.py
@@ -331,136 +331,85 @@
 UNITS = (
     (0, 0, 0, 0, 0, 0, 0, 0),
     (0, 0, 0, 0, 0, 0, 0, 0),
-    (0, 0, 16, 16, 18, 19, 20, 21),
-    (0, 0, 0, 18, 19, 27, 21, 22),
-    (0, 0, 0, 0, 16, 20, 18, 19),
-    (0, 0, 0, 0, 0, 28, 28, 20),
-    (0, 0, 0, 0, 0, 18, 19, 0),
-    (0, 0, 0, 0, 0, 16, 0, 0),
-    (0, 16, 17, 17, 17, 17, 17, 18),
-    (0, 0, 24, 26, 27, 26, 26, 28),
-    (0, 0, 0, 24, 26, 24, 29, 29),
-    (0, 0, 0, 0, 25, 0, 25, 27),
-    (0, 0, 0, 0, 0, 0, 0, 30),
-    (0, 24, 25, 25, 24, 25, 27, 26),
+    (0, 0, 48, 49, 50, 51, 52, 51),
+    (0, 0, 0, 50, 51, 52, 50, 52),
+    (0, 0, 0, 0, 48, 50, 53, 54),
+    (0, 0, 0, 0, 0, 48, 51, 53),
+    (0, 48, 49, 48, 49, 49, 49, 50),
+    (0, 0, 25, 26, 26, 27, 26, 29),
+    (0, 0, 0, 25, 24, 28, 29, 30),
+    (0, 0, 0, 0, 25, 25, 28, 28),
+    (0, 0, 0, 0, 0, 26, 27, 27),
+    (0, 24, 24, 24, 27, 24, 25, 26),
 )
 EVENTS = (
     (
-        (2152, 2209, 2170, 2091, 2172, 2101, 2118, 0),
-        (2144, 2217, 2154, 2083, 0, 2085, 0, 0),
-        (0, 0, 2146, 2099, 0, 2093, 0, 0),
-        (0, 0, 2144, 0, 0, 0, 0, 0),
-        (0, 0, 2152, 0, 0, 0, 0, 0),
-    ),
-    (
-        (0, 0, 0, 2107, 2148, 2147, 2140, 0),
-        (0, 0, 0, 0, 2164, 0, 2116, 0),
-        (0, 0, 0, 0, 2156, 0, 0, 0),
-    ),
-    (
-        (2160, 2233, 2081, 2089, 0, 2155, 2126, 2133),
-        (0, 0, 2136, 0, 0, 0, 0, 0),
-    ),
-    (
-        (0, 0, 0, 2058, 2154, 2109, 0, 2054),
-        (0, 0, 0, 2050, 2112, 2163, 0, 2117),
-        (0, 0, 0, 2048, 2146, 0, 0, 0),
-        (0, 0, 0, 2074, 0, 0, 0, 0),
-        (0, 0, 0, 2105, 0, 0, 0, 0),
-        (0, 0, 0, 2088, 0, 0, 0, 0),
-    ),
-    (
-        (2168, 2056, 0, 0, 2170, 2060, 2124, 2125),
-        (0, 0, 0, 0, 0, 2052, 2058, 2052),
-        (0, 0, 0, 0, 0, 2171, 0, 2115),
-    ),
-    (
-        (0, 2225, 2089, 2104, 2056, 0, 2053, 2076),
-        (0, 0, 0, 0, 2059, 0, 2069, 0),
-        (0, 0, 0, 0, 2051, 0, 0, 0),
-    ),
-    (
-        (0, 2048, 2162, 0, 2145, 0, 2132, 2062),
-        (0, 0, 0, 0, 0, 0, 2114, 2123),
-        (0, 0, 0, 0, 0, 0, 2061, 0),
-    ),
-    (
-        (0, 0, 0, 0, 0, 0, 0, 2060),
-        (0, 0, 0, 0, 0, 0, 0, 2141),
-    ),
-    (
-        (0, 0, 0, 2065, 0, 2076, 0, 0),
-    ),
-    (
-        (0, 0, 0, 2049, 2089, 0, 2134, 0),
+        (2144, 2081, 2146, 2091, 2148, 2101, 2126, 0),
+        (2152, 2217, 2154, 2083, 2156, 2093, 2142, 0),
+        (0, 0, 2170, 0, 2164, 2155, 2116, 0),
+        (0, 0, 0, 0, 2154, 2085, 0, 0),
+        (0, 0, 0, 0, 2146, 0, 0, 0),
+    ),
+    (
+        (2160, 0, 0, 2273, 2170, 2060, 2124, 2133),
+        (0, 0, 0, 2107, 2048, 0, 2118, 2125),
+        (0, 0, 0, 2074, 0, 0, 0, 2123),
+        (0, 0, 0, 0, 0, 0, 0, 2078),
+    ),
+    (
+        (2168, 2105, 2144, 2169, 2120, 2147, 2122, 2117),
+        (0, 0, 2152, 2099, 2172, 2109, 2114, 2052),
+        (0, 0, 2162, 2050, 2081, 2171, 0, 2062),
+        (0, 0, 2089, 2058, 0, 2049, 0, 2115),
+        (0, 0, 0, 2080, 0, 2068, 0, 2054),
+        (0, 0, 0, 2056, 0, 0, 0, 2060),
+        (0, 0, 0, 2057, 0, 0, 0, 0),
+        (0, 0, 0, 2161, 0, 0, 0, 0),
+    ),
+    (
+        (0, 2097, 2049, 0, 2059, 2052, 2132, 0),
+        (0, 0, 0, 0, 2153, 2137, 2061, 0),
+        (0, 0, 0, 0, 2051, 2058, 2134, 0),
+    ),
+    (
+        (0, 2048, 2168, 0, 2162, 2050, 2059, 0),
+        (0, 0, 0, 0, 0, 2163, 2053, 0),
+    ),
+    (
+        (0, 2056, 2160, 0, 0, 2048, 2074, 2141),
+        (0, 0, 0, 0, 0, 2056, 2140, 2139),
+        (0, 0, 0, 0, 0, 2106, 2049, 2050),
+        (0, 0, 0, 0, 0, 0, 2051, 0),
+    ),
+    (
+        (0, 0, 0, 0, 0, 2057, 2057, 2058),
+    ),
+    (
+        (0, 2064, 2097, 2096, 2105, 2076, 2130, 2131),
+        (0, 0, 2073, 2066, 2072, 2064, 2069, 2070),
+        (0, 0, 0, 2104, 2097, 0, 0, 2068),
+    ),
+    (
+        (0, 2072, 0, 0, 2064, 2065, 2077, 0),
         (0, 0, 0, 0, 2067, 0, 0, 0),
-        (0, 0, 0, 0, 2162, 0, 0, 0),
-    ),
-    (
-        (0, 0, 0, 0, 0, 2090, 0, 2139),
-        (0, 0, 0, 0, 0, 2137, 0, 0),
-        (0, 0, 0, 0, 0, 2068, 0, 0),
-        (0, 0, 0, 0, 0, 2048, 0, 0),
-    ),
-    (
-        (0, 0, 0, 0, 0, 0, 0, 2131),
-        (0, 0, 0, 0, 0, 0, 0, 2050),
-        (0, 0, 0, 0, 0, 0, 0, 2068),
-    ),
-    (
-        (0, 0, 0, 0, 0, 2050, 2051, 2058),
-        (0, 0, 0, 0, 0, 2056, 2142, 0),
-        (0, 0, 0, 0, 0, 0, 2059, 0),
-    ),
-    (),
-    (
-        (0, 0, 0, 0, 0, 0, 2057, 0),
-    ),
-    (
-        (0, 0, 0, 0, 0, 0, 2049, 0),
-    ),
-    (
-        (0, 0, 0, 0, 0, 2057, 0, 0),
-        (0, 0, 0, 0, 0, 2074, 0, 0),
-        (0, 0, 0, 0, 0, 2136, 0, 0),
-        (0, 0, 0, 0, 0, 2049, 0, 0),
-    ),
-    (
-        (0, 0, 2160, 0, 2075, 2064, 2138, 0),
-    ),
-    (
-        (0, 2072, 0, 2066, 2128, 2066, 2130, 0),
-        (0, 0, 0, 2064, 2105, 0, 2077, 0),
-    ),
-    (
-        (0, 2064, 0, 0, 0, 0, 0, 0),
-    ),
-    (
-        (0, 0, 2097, 0, 2161, 0, 2075, 0),
+        (0, 0, 0, 0, 2075, 0, 0, 0),
+    ),
+    (
+        (0, 0, 0, 0, 0, 2072, 0, 2076),
+        (0, 0, 0, 0, 0, 2066, 0, 0),
+    ),
+    (
+        (0, 0, 0, 0, 0, 0, 2065, 2074),
+        (0, 0, 0, 0, 0, 0, 2075, 0),
         (0, 0, 0, 0, 0, 0, 2073, 0),
-    ),
-    (
-        (0, 0, 2073, 0, 0, 0, 0, 0),
-    ),
-    (
-        (0, 0, 0, 0, 0, 2065, 2067, 0),
-        (0, 0, 0, 0, 0, 0, 2065, 0),
-    ),
-    (
-        (0, 0, 0, 0, 2072, 0, 0, 2070),
-    ),
-    (
-        (0, 0, 0, 0, 0, 0, 0, 2078),
-        (0, 0, 0, 0, 0, 0, 0, 2074),
+        (0, 0, 0, 0, 0, 0, 2067, 0),
     ),
     (
         (0, 0, 0, 0, 0, 0, 0, 2066),
     ),
-    (),
-    (),
     (),
 )
-LAST = (8, 13)
+LAST = (6, 11)
 
 
 def targets(code, me):
@@ -593,23 +542,24 @@
                         def _():
                             seg_copy(b, way, to).wait_send()
 
-    def one(g, h, k_ref, v_ref, first):
-        i = g * per_group + h
-        scores = lax.dot_general(q_ref[i], k_ref[...], (((1,), (1,)), ((), ())),
+    def several(b, g, hs, first):
+        count = len(hs)
+        span = pl.ds(g * per_group + hs[0], count)
+        scores = lax.dot_general(q_ref[span].reshape(count * rows, head), buf[b, g, 0], (((1,), (1,)), ((), ())),
                                  preferred_element_type=jnp.float32)
-        scores = scores * const + bias[...]
-        high = jnp.broadcast_to(jnp.max(scores, axis=1, keepdims=True), (rows, head))
+        scores = scores * const + jnp.concatenate([bias[...]] * count, axis=0)
+        high = jnp.broadcast_to(jnp.max(scores, axis=1, keepdims=True), (count * rows, head))
         if not first:
-            old = top[i]
+            old = top[span].reshape(count * rows, head)
             high = jnp.maximum(old, high)
         weights = jnp.exp2(scores - jnp.concatenate([high] * (rows // head), axis=1)).astype(jnp.bfloat16)
-        v = jnp.concatenate([v_ref[...], jnp.ones((rows, head), jnp.bfloat16)], axis=1)
+        v = jnp.concatenate([buf[b, g, 1], jnp.ones((rows, head), jnp.bfloat16)], axis=1)
         mixed = jnp.dot(weights, v, preferred_element_type=jnp.float32)
         if not first:
             factor = jnp.exp2(old - high)
-            mixed = acc[i] * jnp.concatenate([factor, factor], axis=1) + mixed
-        acc[i] = mixed
-        top[i] = high
+            mixed = acc[span].reshape(count * rows, 2 * head) * jnp.concatenate([factor, factor], axis=1) + mixed
+        acc[span] = mixed.reshape(count, rows, 2 * head)
+        top[span] = high.reshape(count, rows, head)
 
     def set_bias(b, first):
         allowed = jnp.concatenate([segcol[...]] * (rows // head), axis=1) == segs[b]
@@ -619,19 +569,16 @@
             allowed = allowed & (c <= r)
         bias[...] = jnp.where(allowed, 0.0, NEG)
 
-    def unit(values, half):
+    def unit(values):
         code = pick(values)
         b, g = code % 8, code // 8 % 2
 
-        @pl.when(code // 16 == 1)
-        def _():
-            if half == 0:
-                set_bias(b, False)
-            for h in halves[half]:
-                one(g, h, buf.at[b, g, 0], buf.at[b, g, 1], False)
-
-    halves = (range(per_group // 2), range(per_group // 2, per_group))
-    per_send = 2
+        @pl.when(code // 16 % 2 == 1)
+        def _():
+            set_bias(b, False)
+            several(b, g, range(per_group), False)
+
+    per_send = per_group // 2
     width = per_send * head
     pieces = per_group // per_send
 
@@ -647,20 +594,18 @@
             device_id_type=MESH,
         )
 
-    def last_unit(values, g, half):
+    def last_unit(values, g):
         code = pick(values)
         b = code % 8
-        live = code // 16 == 1
-
-        if half == 0:
+        live = code // 16 % 2 == 1
+
+        @pl.when(live)
+        def _():
+            set_bias(b, False)
+        for p in range(pieces):
             @pl.when(live)
             def _():
-                set_bias(b, False)
-        for p in range(half * pieces // 2, (half + 1) * pieces // 2):
-            @pl.when(live)
-            def _():
-                for h in range(per_send):
-                    one(g, p * per_send + h, buf.at[b, g, 0], buf.at[b, g, 1], False)
+                several(b, g, range(p * per_send, (p + 1) * per_send), False)
             c = g * pieces + p
             for h in range(per_send):
                 i = g * per_group + p * per_send + h
@@ -677,20 +622,18 @@
     segcol[...] = jnp.transpose(jnp.broadcast_to(segs[me], (head, rows)))
     set_bias(me, True)
     for step, values in enumerate(UNITS):
-        for half in range(2):
-            if step + half > 0:
-                for slot in EVENTS[2 * step + half]:
-                    event(slot)
-            if step < groups:
-                for h in halves[half]:
-                    q_ref[step * per_group + h] = q_raw[:, step * per_group + h, :]
-                for h in halves[half]:
-                    one(step, h, buf.at[me, step, 0], buf.at[me, step, 1], True)
-            elif step in LAST:
-                last_unit(values, LAST.index(step), half)
-            else:
-                unit(values, half)
-    for slot in EVENTS[2 * len(UNITS)]:
+        if step > 0:
+            for slot in EVENTS[step]:
+                event(slot)
+        if step < groups:
+            for h in range(step * per_group, (step + 1) * per_group):
+                q_ref[h] = q_raw[:, h, :]
+            several(me, step, range(per_group), True)
+        elif step in LAST:
+            last_unit(values, LAST.index(step))
+        else:
+            unit(values)
+    for slot in EVENTS[len(UNITS)]:
         event(slot)
 
     for group in EVENTS:
@@ -707,7 +650,7 @@
     per_group = heads // groups
     n = lax.axis_size("ctx")
     tp = lax.axis_size("tp")
-    chunks = groups * per_group // 2
+    chunks = groups * 2
     hbm = pl.BlockSpec(memory_space=pltpu.HBM)
     dma = pltpu.SemaphoreType.DMA
     cfg = (n, tp, groups, per_group, rows, head)

time: 35 us -> 32.4 us (0.926)
  Pallas kernels: 33.8 us -> 31.2 us
    pallas_call x1, Pallas kernels: 33.8 us -> 31.2 us  [planned(): pl.pallas_call(functools.partial(planned_kernel, cfg), out_shape=pltpu.VM...]
where the time goes in v3:
time: 32.4 us; the launch traced here: 32.2 us
  Pallas kernels  31.2 us (96%)
  local copies, waits for them, and re-layouts  0.97 us (3%)
    pallas_call x1, Pallas kernels, planned(): pl.pallas_call(functools.partial(planned_kernel, cfg), out_shape=pltpu.VM...  31.2 us
    unnamed x1, local copies, waits for them, and re-layouts  0.97 us

profile of v3, /device:TPU:25, one launch (start us, length us, event | category | flops | bytes accessed | tf_op | source)
XLA Modules:
  0.0 32.2 jit_solution(16873050894734113696)
XLA Ops:
  0.0 31.2 %shard_map.46 = bf16[64,8192]{1,0:T(8,128)(2,1)S(1)} custom-call(bf16[256,16,128]{2,1,0:T(8,128)(2,1)} %q_hbm.1, bf16[256,2,128]{2,1,0:T(2,128)(2,1)} %k_hbm.1, bf16[256,2,128]{2,1,0:T(2,128)(2,1)} %v_hbm.1, s32[1,256]{1,0:T(1,128)} %bitcast.1), custom_call_target="tpu_custom_call" | custom-call | tf_op jit(solution)/shard_map/pallas_call | solution.py:657
  31.2 1.0 %copy.6 = bf16[64,8192]{1,0:T(8,128)(2,1)} copy(bf16[64,8192]{1,0:T(8,128)(2,1)S(1)} %shard_map.46) | data formatting | bytes 2097152

commit v4 on v3

--- a/solution.py
+++ b/solution.py
@@ -331,85 +331,98 @@
 UNITS = (
     (0, 0, 0, 0, 0, 0, 0, 0),
     (0, 0, 0, 0, 0, 0, 0, 0),
-    (0, 0, 48, 49, 50, 51, 52, 51),
-    (0, 0, 0, 50, 51, 52, 50, 52),
-    (0, 0, 0, 0, 48, 50, 53, 54),
-    (0, 0, 0, 0, 0, 48, 51, 53),
-    (0, 48, 49, 48, 49, 49, 49, 50),
-    (0, 0, 25, 26, 26, 27, 26, 29),
-    (0, 0, 0, 25, 24, 28, 29, 30),
-    (0, 0, 0, 0, 25, 25, 28, 28),
-    (0, 0, 0, 0, 0, 26, 27, 27),
-    (0, 24, 24, 24, 27, 24, 25, 26),
+    (0, 0, 49, 50, 49, 51, 52, 53),
+    (0, 0, 0, 57, 51, 50, 50, 51),
+    (0, 0, 0, 17, 50, 52, 53, 54),
+    (0, 0, 0, 0, 0, 27, 51, 52),
+    (0, 0, 0, 0, 0, 49, 0, 0),
+    (0, 48, 48, 48, 48, 48, 49, 50),
+    (0, 0, 24, 26, 26, 26, 29, 27),
+    (0, 0, 0, 0, 25, 25, 28, 29),
+    (0, 0, 0, 0, 24, 24, 26, 28),
+    (0, 0, 0, 0, 0, 0, 27, 30),
+    (0, 24, 25, 24, 27, 28, 25, 26),
 )
 EVENTS = (
     (
-        (2144, 2081, 2146, 2091, 2148, 2101, 2126, 0),
-        (2152, 2217, 2154, 2083, 2156, 2093, 2142, 0),
-        (0, 0, 2170, 0, 2164, 2155, 2116, 0),
-        (0, 0, 0, 0, 2154, 2085, 0, 0),
+        (2144, 2081, 2154, 2083, 2156, 2085, 2118, 0),
+        (2152, 2217, 2146, 2091, 2148, 2093, 2134, 0),
+        (0, 0, 0, 0, 2164, 2147, 0, 0),
+        (0, 0, 0, 0, 2154, 2155, 0, 0),
         (0, 0, 0, 0, 2146, 0, 0, 0),
-    ),
-    (
-        (2160, 0, 0, 2273, 2170, 2060, 2124, 2133),
-        (0, 0, 0, 2107, 2048, 0, 2118, 2125),
-        (0, 0, 0, 2074, 0, 0, 0, 2123),
-        (0, 0, 0, 0, 0, 0, 0, 2078),
-    ),
-    (
-        (2168, 2105, 2144, 2169, 2120, 2147, 2122, 2117),
-        (0, 0, 2152, 2099, 2172, 2109, 2114, 2052),
-        (0, 0, 2162, 2050, 2081, 2171, 0, 2062),
-        (0, 0, 2089, 2058, 0, 2049, 0, 2115),
-        (0, 0, 0, 2080, 0, 2068, 0, 2054),
-        (0, 0, 0, 2056, 0, 0, 0, 2060),
+        (0, 0, 0, 0, 2170, 0, 0, 0),
+        (0, 0, 0, 0, 2172, 0, 0, 0),
+    ),
+    (
+        (2168, 0, 2170, 2273, 0, 2060, 2126, 0),
+        (0, 0, 0, 2107, 0, 2101, 2116, 0),
+        (0, 0, 0, 2050, 0, 2109, 2124, 0),
         (0, 0, 0, 2057, 0, 0, 0, 0),
-        (0, 0, 0, 2161, 0, 0, 0, 0),
-    ),
-    (
-        (0, 2097, 2049, 0, 2059, 2052, 2132, 0),
-        (0, 0, 0, 0, 2153, 2137, 2061, 0),
-        (0, 0, 0, 0, 2051, 2058, 2134, 0),
-    ),
-    (
-        (0, 2048, 2168, 0, 2162, 2050, 2059, 0),
-        (0, 0, 0, 0, 0, 2163, 2053, 0),
-    ),
-    (
-        (0, 2056, 2160, 0, 0, 2048, 2074, 2141),
-        (0, 0, 0, 0, 0, 2056, 2140, 2139),
-        (0, 0, 0, 0, 0, 2106, 2049, 2050),
+    ),
+    (
+        (2160, 2105, 2152, 2058, 2153, 2052, 2122, 2117),
+        (0, 0, 2144, 2169, 2081, 0, 2114, 2054),
+        (0, 0, 2089, 2099, 2048, 0, 0, 2125),
+        (0, 0, 2162, 2074, 2120, 0, 0, 2115),
+        (0, 0, 2049, 2161, 0, 0, 0, 2070),
+        (0, 0, 0, 2056, 0, 0, 0, 2123),
+        (0, 0, 0, 0, 0, 0, 0, 2052),
+    ),
+    (
+        (0, 2056, 0, 0, 2059, 2171, 2132, 2062),
+        (0, 0, 0, 0, 2051, 2058, 2053, 0),
+        (0, 0, 0, 0, 0, 2050, 0, 0),
+    ),
+    (
+        (0, 2048, 0, 2080, 2162, 2137, 2061, 2133),
         (0, 0, 0, 0, 0, 0, 2051, 0),
-    ),
-    (
-        (0, 0, 0, 0, 0, 2057, 2057, 2058),
-    ),
-    (
-        (0, 2064, 2097, 2096, 2105, 2076, 2130, 2131),
-        (0, 0, 2073, 2066, 2072, 2064, 2069, 2070),
-        (0, 0, 0, 2104, 2097, 0, 0, 2068),
-    ),
-    (
-        (0, 2072, 0, 0, 2064, 2065, 2077, 0),
-        (0, 0, 0, 0, 2067, 0, 0, 0),
+        (0, 0, 0, 0, 0, 0, 2142, 0),
+        (0, 0, 0, 0, 0, 0, 2140, 0),
+    ),
+    (
+        (0, 0, 0, 0, 0, 2163, 2074, 2141),
+        (0, 0, 0, 0, 0, 0, 2059, 2060),
+        (0, 0, 0, 0, 0, 0, 0, 2058),
+    ),
+    (
+        (0, 0, 0, 0, 0, 2106, 2057, 2050),
+        (0, 0, 0, 0, 0, 2068, 2069, 0),
+        (0, 0, 0, 0, 0, 2049, 0, 0),
+        (0, 0, 0, 0, 0, 2057, 0, 0),
+    ),
+    (
+        (0, 0, 0, 0, 0, 2065, 2049, 0),
+        (0, 0, 0, 0, 0, 2076, 0, 0),
+        (0, 0, 0, 0, 0, 2048, 0, 0),
+        (0, 0, 0, 0, 0, 2056, 0, 0),
+    ),
+    (
+        (0, 2097, 2168, 2104, 2064, 2066, 2077, 2139),
+        (0, 0, 2073, 2066, 2105, 0, 2130, 2131),
+        (0, 0, 2160, 2096, 0, 0, 0, 2078),
+        (0, 0, 2097, 0, 0, 0, 0, 0),
+    ),
+    (
+        (0, 2072, 0, 0, 2097, 0, 0, 0),
+        (0, 0, 0, 0, 2072, 0, 0, 0),
         (0, 0, 0, 0, 2075, 0, 0, 0),
     ),
     (
-        (0, 0, 0, 0, 0, 2072, 0, 2076),
-        (0, 0, 0, 0, 0, 2066, 0, 0),
-    ),
-    (
-        (0, 0, 0, 0, 0, 0, 2065, 2074),
-        (0, 0, 0, 0, 0, 0, 2075, 0),
+        (0, 2064, 0, 0, 2067, 2072, 0, 2068),
+        (0, 0, 0, 0, 0, 2064, 0, 2076),
+    ),
+    (
+        (0, 0, 0, 0, 0, 0, 2075, 2074),
         (0, 0, 0, 0, 0, 0, 2073, 0),
         (0, 0, 0, 0, 0, 0, 2067, 0),
+        (0, 0, 0, 0, 0, 0, 2065, 0),
     ),
     (
         (0, 0, 0, 0, 0, 0, 0, 2066),
     ),
     (),
 )
-LAST = (6, 11)
+LAST = (7, 12)
 
 
 def targets(code, me):
@@ -547,7 +560,7 @@
         span = pl.ds(g * per_group + hs[0], count)
         scores = lax.dot_general(q_ref[span].reshape(count * rows, head), buf[b, g, 0], (((1,), (1,)), ((), ())),
                                  preferred_element_type=jnp.float32)
-        scores = scores * const + jnp.concatenate([bias[...]] * count, axis=0)
+        scores = scores * const + jnp.concatenate([bias[b]] * count, axis=0)
         high = jnp.broadcast_to(jnp.max(scores, axis=1, keepdims=True), (count * rows, head))
         if not first:
             old = top[span].reshape(count * rows, head)
@@ -567,15 +580,18 @@
             r = lax.broadcasted_iota(jnp.int32, (rows, rows), 0)
             c = lax.broadcasted_iota(jnp.int32, (rows, rows), 1)
             allowed = allowed & (c <= r)
-        bias[...] = jnp.where(allowed, 0.0, NEG)
+        bias[b] = jnp.where(allowed, 0.0, NEG)
 
     def unit(values):
         code = pick(values)
         b, g = code % 8, code // 8 % 2
 
+        @pl.when(code // 32 == 1)
+        def _():
+            set_bias(b, False)
+
         @pl.when(code // 16 % 2 == 1)
         def _():
-            set_bias(b, False)
             several(b, g, range(per_group), False)
 
     per_send = per_group // 2
@@ -599,7 +615,7 @@
         b = code % 8
         live = code // 16 % 2 == 1
 
-        @pl.when(live)
+        @pl.when(code // 32 == 1)
         def _():
             set_bias(b, False)
         for p in range(pieces):
@@ -666,7 +682,7 @@
             pltpu.VMEM((n, groups, 2, rows, head), jnp.bfloat16),
             pltpu.VMEM((n, 1, rows), jnp.int32),
             pltpu.VMEM((rows, head), jnp.int32),
-            pltpu.VMEM((rows, rows), jnp.float32),
+            pltpu.VMEM((n, rows, rows), jnp.float32),
             pltpu.VMEM((heads, rows, 2 * head), jnp.float32),
             pltpu.VMEM((heads, rows, head), jnp.float32),
             pltpu.VMEM((rows, heads * head), jnp.bfloat16),

time: 32.4 us -> 32.2 us (level)
  Pallas kernels: 31.2 us -> 30.8 us
    pallas_call x1, Pallas kernels: 31.2 us -> 30.8 us  [planned(): pl.pallas_call(functools.partial(planned_kernel, cfg), out_shape=pltpu.VM...]
where the time goes in v4:
time: 32.2 us; the launch traced here: 31.8 us
  Pallas kernels  30.8 us (96%)
  local copies, waits for them, and re-layouts  0.97 us (3%)
    pallas_call x1, Pallas kernels, planned(): pl.pallas_call(functools.partial(planned_kernel, cfg), out_shape=pltpu.VM...  30.8 us
    unnamed x1, local copies, waits for them, and re-layouts  0.97 us

profile of v4, /device:TPU:25, one launch (start us, length us, event | category | flops | bytes accessed | tf_op | source)
XLA Modules:
  0.0 31.8 jit_solution(16465918199784642933)
XLA Ops:
  0.0 30.8 %shard_map.46 = bf16[64,8192]{1,0:T(8,128)(2,1)S(1)} custom-call(bf16[256,16,128]{2,1,0:T(8,128)(2,1)} %q_hbm.1, bf16[256,2,128]{2,1,0:T(2,128)(2,1)} %k_hbm.1, bf16[256,2,128]{2,1,0:T(2,128)(2,1)} %v_hbm.1, s32[1,256]{1,0:T(1,128)} %bitcast.1), custom_call_target="tpu_custom_call" | custom-call | tf_op jit(solution)/shard_map/pallas_call | solution.py:673
  30.8 1.0 %copy.6 = bf16[64,8192]{1,0:T(8,128)(2,1)} copy(bf16[64,8192]{1,0:T(8,128)(2,1)S(1)} %shard_map.46) | data formatting | bytes 2097152
